TPU v7x, 32 devices: a whole 2x2x4 slice. The times are simulated.
32 devices in a mesh: layer: 4 (over y, x), row: 2 (over core), col: 4 (over z).
Axes of the slice: x: 2, y: 2, z: 4, core: 2. Of those that a mesh axis runs over, the one named last changes fastest.
Arguments:
- hidden: bfloat16 [384, 2304], P(('layer', 'row')), may hold values from -60 to 60
- embedding: bfloat16 [16384, 2304], P(('row', 'col'), 'layer'), may hold values from -0.3 to 0.3
- teacher: bfloat16 [384, 16384], P('layer', ('row', 'col')), may hold values from -80 to 240
Outputs:
- grad_embedding: float32 [16384, 2304], P(('row', 'col'), 'layer')
- grad_hidden: float32 [384, 2304], P(('layer', 'row', 'col'))
All inputs are finite; a program needn't handle non-finite values.
Results may differ from a plain program's by a relative error of at most 0.0041.
Values may be sent and summed in bfloat16 or wider, within the bound.
A program may use at most 192 MiB of HBM per device.

v0:
```python
import jax
import jax.numpy as jnp
from jax import lax
from jax.sharding import PartitionSpec as P

LOSS_SCALE = 256


def local(hidden, embedding, teacher):
    token_rows = lax.all_gather(hidden, "row", axis=0, tiled=True)
    width_part = lax.all_to_all(token_rows, "layer", split_axis=1, concat_axis=0, tiled=True)
    logits = lax.psum_scatter(
        lax.dot_general(
            width_part, embedding, (((1,), (1,)), ((), ())), preferred_element_type=jnp.float32
        ),
        "layer",
        scatter_dimension=0,
        tiled=True,
    )
    teach_f = teacher.astype(jnp.float32)
    top_s, top_t = lax.pmax((jnp.max(logits, axis=1), jnp.max(teach_f, axis=1)), ("row", "col"))
    part_s = jnp.sum(jnp.exp(logits - top_s[:, None]), axis=1)
    part_t = jnp.sum(jnp.exp(teach_f - top_t[:, None]), axis=1)
    sum_s, sum_t = lax.psum((part_s, part_t), ("row", "col"))
    lse_s = top_s + jnp.log(sum_s)
    lse_t = top_t + jnp.log(sum_t)
    prob_s = jnp.exp(logits - lse_s[:, None])
    prob_t = jnp.exp(teach_f - lse_t[:, None])
    grads = ((prob_s - prob_t) * LOSS_SCALE).astype(jnp.bfloat16)
    grad_piece = lax.all_gather(grads, "layer", axis=0, tiled=True)
    embed_acc = lax.dot_general(
        grad_piece, width_part, (((0,), (0,)), ((), ())), preferred_element_type=jnp.float32
    )
    hidden_piece = jnp.dot(grad_piece, embedding, preferred_element_type=jnp.float32)
    hidden_terms = lax.all_to_all(hidden_piece, "layer", split_axis=0, concat_axis=1, tiled=True)
    grad_hidden = lax.psum_scatter(hidden_terms, ("row", "col"), scatter_dimension=0, tiled=True)
    return (embed_acc, grad_hidden)


def solution(mesh):
    placed = (P(("layer", "row"), None), P(("row", "col"), "layer"), P("layer", ("row", "col")))
    return jax.shard_map(
        local,
        mesh=mesh,
        in_specs=placed,
        out_specs=(P(("row", "col"), "layer"), P(("layer", "row", "col"), None)),
        check_vma=False,
    )
```

profile of v0, /device:TPU:1, one launch (start us, length us, event | category | flops | bytes accessed | tf_op | source)
XLA Modules:
  0.0 216.0 jit_solution(10763876937868347929)
XLA Ops:
  7.2 2.5 %all_gather.6 = bf16[96,2304]{1,0:T(8,128)(2,1)S(1)} all-gather(bf16[48,2304]{1,0:T(8,128)(2,1)} %param.3), channel_id=1, replica_groups=mesh['layer'=4,'row'=2,'col'=4] {'row'}, dimensions={0}, use_global_device_ids=true | all-gather | bytes 663552 | tf_op jit(solution)/shard_map/all_gather | solution.py:10
  10.3 11.5 %all_to_all.38 = bf16[96,4,576]{2,0,1:T(8,128)(2,1)S(1)} all-to-all(bf16[96,4,576]{2,0,1:T(8,128)(2,1)S(1)} %copy.11), channel_id=1, replica_groups=mesh['layer'=4,'row'=2,'col'=4] {'layer'}, dimensions={1} | all-to-all | bytes 884736 | tf_op jit(solution)/shard_map/all_to_all | solution.py:11
  21.8 0.8 copy-done.2
  22.6 3.1 %fusion.7 = f32[384,2048]{1,0:T(8,128)} fusion(bf16[384,576]{1,0:T(8,128)(2,1)S(1)} %bitcast.14, bf16[2048,576]{0,1:T(8,128)(2,1)S(1)} %copy-done), kind=kOutput, calls=%fused_computation.12 | convolution fusion | flops 905969664 | bytes 5947392 | tf_op jit(solution)/shard_map/dot_general | solution.py:13
  25.8 0.9 copy-done.5
  26.8 43.8 %reduce-scatter.4.cloned.1.call-done = f32[96,2048]{1,0:T(8,128)} async-done(((f32[384,2048]{1,0:T(8,128)}), f32[96,2048]{1,0:T(8,128)}) %reduce-scatter.4.cloned.1.call-update) | async-done | bytes 786448 | tf_op jit(solution)/shard_map/reduce_scatter | solution.py:12
  70.6 1.3 reduce_max.23
  72.0 17.8 %all-reduce.3 = (f32[96]{0:T(128)S(1)}, f32[96]{0:T(128)S(1)}) all-reduce(bf16[96]{0:T(256)(128)(2,1)S(1)} %reduce_max.24, f32[96]{0:T(128)S(1)} %reduce_max.23), channel_id=1, replica_groups=mesh['layer'=4,'row'=2,'col'=4] {'row','col'}, use_global_device_ids=true, to_apply=%region_6.0 | all-reduce | flops 192 | bytes 1344 | tf_op jit(solution)/shard_map/pmax | solution.py:21
  89.8 1.5 fusion.2
  91.4 14.2 %all-reduce.2 = (f32[96]{0:T(128)}, f32[96]{0:T(128)}) all-reduce(f32[96]{0:T(128)S(1)} %get-tuple-element.6, f32[96]{0:T(128)S(1)} %get-tuple-element.7), channel_id=1, replica_groups=mesh['layer'=4,'row'=2,'col'=4] {'row','col'}, use_global_device_ids=true, to_apply=%region_8.0 | all-reduce | flops 192 | bytes 1536 | tf_op jit(solution)/shard_map/psum | solution.py:24
  106.9 1.1 fusion.6
  108.0 29.8 %all-gather.2.cloned.1.call-done = bf16[384,2048]{1,0:T(8,128)(2,1)} async-done(((bf16[96,2048]{1,0:T(8,128)(2,1)}), bf16[384,2048]{1,0:T(8,128)(2,1)}) %all-gather.2.cloned.1.call-update) | async-done | bytes 1572880 | tf_op jit(solution)/shard_map/all_gather | solution.py:30
  137.8 3.8 %fusion.9 = f32[384,576]{1,0:T(8,128)} fusion(bf16[384,2048]{1,0:T(8,128)(2,1)} %all-gather.2.cloned.1.call-done, bf16[2048,576]{0,1:T(8,128)(2,1)S(1)} %copy-done), kind=kOutput, calls=%fused_computation.14 | convolution fusion | flops 905969664 | bytes 4816896 | tf_op jit(solution)/shard_map/dot_general | solution.py:34
  141.6 3.5 %all-to-all-start.1 = ((f32[4,96,576]{2,1,0:T(8,128)}), f32[4,96,576]{2,1,0:T(8,128)S(1)}, u32[]{:S(2)}, u32[]{:S(2)}) async-start(f32[4,96,576]{2,1,0:T(8,128)} %bitcast.17), calls=%async_computation.2 | async-start | bytes 1966080 | tf_op jit(solution)/shard_map/all_to_all | solution.py:35
  146.3 11.2 %all-to-all-done.1 = f32[4,96,576]{2,1,0:T(8,128)S(1)} async-done(((f32[4,96,576]{2,1,0:T(8,128)}), f32[4,96,576]{2,1,0:T(8,128)S(1)}, u32[]{:S(2)}, u32[]{:S(2)}) %all-to-all-start.1) | async-done | bytes 884768 | tf_op jit(solution)/shard_map/all_to_all | solution.py:35
  157.5 0.9 copy-done.4
  158.4 2.8 %copy.13 = f32[96,4,576]{2,1,0:T(4,128)} copy(f32[96,4,576]{2,0,1:T(8,128)} %bitcast.16) | data formatting | bytes 1769472 | tf_op jit(solution)/shard_map/all_to_all | solution.py:35
  161.3 2.7 %all_to_all.35 = f32[96,2304]{1,0:T(8,128)} reshape(f32[96,4,576]{2,1,0:T(4,128)} %copy.13) | data formatting | bytes 1769472 | tf_op jit(solution)/shard_map/all_to_all | solution.py:35
  164.0 32.7 %fusion = f32[16,2304]{1,0:T(8,128)S(1)} fusion(f32[96,2304]{1,0:T(8,128)} %all_to_all.35), kind=kCustom, calls=%all-reduce-scatter | all-reduce-scatter fusion | flops 294913 | bytes 1032704
  196.7 1.9 collective-permute-start
  198.6 2.4 %collective-permute-start.1 = (f32[12,2304]{1,0:T(8,128)S(1)}, f32[12,2304]{1,0:T(8,128)S(1)}, u32[]{:S(2)}, u32[]{:S(2)}) collective-permute-start(f32[12,2304]{1,0:T(8,128)S(1)} %slice), channel_id=1, source_target_pairs={{0,2},{1,3},{2,4},{3,5},{4,6},{5,7},{8,10},{9,11},{10,12},{11,13},... | collective-permute-start | bytes 331784
  201.0 5.0 %fusion.8 = f32[2048,576]{0,1:T(8,128)} fusion(bf16[384,2048]{1,0:T(8,128)(2,1)} %all-gather.2.cloned.1.call-done, bf16[384,576]{1,0:T(8,128)(2,1)S(1)} %bitcast.15), kind=kOutput, calls=%fused_computation.13 | convolution fusion | flops 905969664 | bytes 6733824 | tf_op jit(solution)/shard_map/dot_general | solution.py:31
  206.1 2.0 collective-permute-done.1
  208.5 0.7 constant_dynamic-slice_fusion
  (24 shorter events, 3.2 us)
Async XLA Ops:
  7.2 15.5 %copy-start = (bf16[2048,576]{0,1:T(8,128)(2,1)S(1)}, bf16[2048,576]{0,1:T(8,128)(2,1)}, u32[]{:S(2)}) copy-start(bf16[2048,576]{0,1:T(8,128)(2,1)} %param.4) | copy-start | bytes 7077892
  7.2 63.5 %reduce-scatter.4.cloned.1.call-start = ((), (), s32[]{:S(2)}) async-start(), calls=%async_computation.3 | async-start | bytes 3932160 | tf_op jit(solution)/shard_map/reduce_scatter | solution.py:12
  21.8 0.8 copy-start.2
  25.7 1.0 copy-start.5
  25.7 112.1 %all-gather.2.cloned.1.call-start = ((), (), s32[]{:S(2)}) async-start(), calls=%async_computation.4 | async-start | bytes 1966080 | tf_op jit(solution)/shard_map/all_gather | solution.py:30
  70.6 36.2 %copy-start.1 = (f32[96,2048]{1,0:T(8,128)S(1)}, f32[96,2048]{1,0:T(8,128)}, u32[]{:S(2)}) copy-start(f32[96,2048]{1,0:T(8,128)} %reduce-scatter.4.cloned.1.call-done) | copy-start | bytes 2359300
  108.0 37.1 %copy-start.6 = (u32[32]{0:T(128)S(1)}, u32[32]{0:T(128)}, u32[]{:S(2)}) copy-start(u32[32]{0:T(128)} %constant.10) | copy-start | bytes 388
  141.6 15.9 %all-to-all-start.1 = ((f32[4,96,576]{2,1,0:T(8,128)}), f32[4,96,576]{2,1,0:T(8,128)S(1)}, u32[]{:S(2)}, u32[]{:S(2)}) async-start(f32[4,96,576]{2,1,0:T(8,128)} %bitcast.17), calls=%async_computation.2 | async-start | bytes 1966080 | tf_op jit(solution)/shard_map/all_to_all | solution.py:35
  157.5 0.9 copy-start.4
  158.4 42.6 %copy-start.3 = (bf16[96,4,576]{2,0,1:T(8,128)(2,1)S(1)}, bf16[96,4,576]{2,0,1:T(8,128)(2,1)}, u32[]{:S(2)}) copy-start(bf16[96,4,576]{2,0,1:T(8,128)(2,1)} %copy-done.2) | copy-start | bytes 1327108
  196.7 11.4 %collective-permute-start = (f32[16,2304]{1,0:T(8,128)S(1)}, f32[16,2304]{1,0:T(8,128)S(1)}, u32[]{:S(2)}, u32[]{:S(2)}) collective-permute-start(f32[16,2304]{1,0:T(8,128)S(1)} %fusion), channel_id=1, source_target_pairs={{0,1},{1,2},{2,3},{3,4},{4,5},{5,6},{6,7},{8,9},{9,10},{10,11},{11... | collective-permute-start | bytes 442376
  198.6 9.5 %collective-permute-start.1 = (f32[12,2304]{1,0:T(8,128)S(1)}, f32[12,2304]{1,0:T(8,128)S(1)}, u32[]{:S(2)}, u32[]{:S(2)}) collective-permute-start(f32[12,2304]{1,0:T(8,128)S(1)} %slice), channel_id=1, source_target_pairs={{0,2},{1,3},{2,4},{3,5},{4,6},{5,7},{8,10},{9,11},{10,12},{11,13},... | collective-permute-start | bytes 331784
Sparse Core Ops, SparseCore 0:
  25.8 44.7 reduce-scatter.3
  108.1 29.6 all-gather.1
where the time goes:
time: 217 us; the launch traced here: 216 us
  waiting for transfers between devices  86.8 us (40%)
  blocking collectives  78.7 us (36%)
  between operations  14.8 us (7%)
  matrix products  11.9 us (5%)
  local copies, waits for them, and re-layouts  10.5 us (5%)
  starting transfers between devices  7.91 us (4%)
  other arithmetic  5.41 us (2%)
    reduce_scatter x1, waiting for transfers between devices, local(): lax.psum_scatter(lax.dot_general(width_part, embedding, (((1,), (1,)), ((...  43.8 us
    unnamed x1, blocking collectives  32.7 us
    all_gather x1, waiting for transfers between devices, local(): grad_piece = lax.all_gather(grads, 'layer', axis=0, tiled=True)  29.8 us
    pmax x1, blocking collectives, local(): lax.pmax((jnp.max(logits, axis=1), jnp.max(teach_f, axis=1)), ('row', 'co...  17.8 us
    psum x1, blocking collectives, local(): sum_s, sum_t = lax.psum((part_s, part_t), ('row', 'col'))  14.2 us
    all_to_all x1, blocking collectives, local(): lax.all_to_all(token_rows, 'layer', split_axis=1, concat_axis=0, tiled=True)  11.5 us
    all_to_all x1, waiting for transfers between devices, local(): lax.all_to_all(hidden_piece, 'layer', split_axis=0, concat_axis=1, tiled=...  11.2 us
    all_to_all x2, local copies, waits for them, and re-layouts, local(): lax.all_to_all(hidden_piece, 'layer', split_axis=0, concat_axis=1, tiled=...  5.53 us
  transfers between devices with their start and end apart: 5, of which 4 were waited for; matrix products, arithmetic and copies ran while one was open for 3% of the time, Pallas kernels for 0%

commit v1 on v0

--- a/solution.py
+++ b/solution.py
@@ -8,7 +8,10 @@
 
 def local(hidden, embedding, teacher):
     token_rows = lax.all_gather(hidden, "row", axis=0, tiled=True)
-    width_part = lax.all_to_all(token_rows, "layer", split_axis=1, concat_axis=0, tiled=True)
+    peers = lax.axis_size("layer")
+    blocks = jnp.stack(jnp.split(token_rows, peers, axis=1), axis=0)
+    blocks = lax.all_to_all(blocks, "layer", split_axis=0, concat_axis=0)
+    width_part = jnp.concatenate(blocks, axis=0)
     logits = lax.psum_scatter(
         lax.dot_general(
             width_part, embedding, (((1,), (1,)), ((), ())), preferred_element_type=jnp.float32

time: 217 us -> 216 us (level)
  no operation moved by 1% of the time
where the time goes in v1:
time: 216 us
  waiting for transfers between devices  86.8 us (40%)
  blocking collectives  78.7 us (36%)
  between operations  14.8 us (7%)
  matrix products  11.9 us (6%)
  local copies, waits for them, and re-layouts  10 us (5%)
  starting transfers between devices  7.91 us (4%)
  other arithmetic  5.51 us (3%)
    reduce_scatter x1, waiting for transfers between devices, local(): lax.psum_scatter(lax.dot_general(width_part, embedding, (((1,), (1,)), ((...  43.8 us
    unnamed x1, blocking collectives  32.7 us
    all_gather x1, waiting for transfers between devices, local(): grad_piece = lax.all_gather(grads, 'layer', axis=0, tiled=True)  29.8 us
    pmax x1, blocking collectives, local(): lax.pmax((jnp.max(logits, axis=1), jnp.max(teach_f, axis=1)), ('row', 'co...  17.8 us
    psum x1, blocking collectives, local(): sum_s, sum_t = lax.psum((part_s, part_t), ('row', 'col'))  14.2 us
    all_to_all x1, blocking collectives, local(): blocks = lax.all_to_all(blocks, 'layer', split_axis=0, concat_axis=0)  11.5 us
    all_to_all x1, waiting for transfers between devices, local(): lax.all_to_all(hidden_piece, 'layer', split_axis=0, concat_axis=1, tiled=...  11.2 us
    all_to_all x2, local copies, waits for them, and re-layouts, local(): lax.all_to_all(hidden_piece, 'layer', split_axis=0, concat_axis=1, tiled=...  5.53 us
  transfers between devices with their start and end apart: 5, of which 4 were waited for; matrix products, arithmetic and copies ran while one was open for 3% of the time, Pallas kernels for 0%

profile of v1, /device:TPU:1, one launch (start us, length us, event | category | flops | bytes accessed | tf_op | source)
XLA Modules:
  0.0 215.6 jit_solution(11910348327639930722)
XLA Ops:
  7.2 2.5 %all_gather.6 = bf16[96,2304]{1,0:T(8,128)(2,1)S(1)} all-gather(bf16[48,2304]{1,0:T(8,128)(2,1)} %param.3), channel_id=1, replica_groups=mesh['layer'=4,'row'=2,'col'=4] {'row'}, dimensions={0}, use_global_device_ids=true | all-gather | bytes 663552 | tf_op jit(solution)/shard_map/all_gather | solution.py:10
  9.9 11.5 %all_to_all.24 = bf16[4,96,576]{2,1,0:T(8,128)(2,1)S(1)} all-to-all(bf16[4,96,576]{2,1,0:T(8,128)(2,1)S(1)} %pad_maximum_fusion), channel_id=1, replica_groups=mesh['layer'=4,'row'=2,'col'=4] {'layer'}, dimensions={0} | all-to-all | bytes 884736 | tf_op jit(solution)/shard_map/all_to_all | solution.py:13
  21.4 0.8 copy-done.2
  22.2 3.1 %fusion.7 = f32[384,2048]{1,0:T(8,128)} fusion(bf16[384,576]{1,0:T(8,128)(2,1)S(1)} %bitcast.20, bf16[2048,576]{0,1:T(8,128)(2,1)S(1)} %copy-done), kind=kOutput, calls=%fused_computation.17 | convolution fusion | flops 905969664 | bytes 5947392 | tf_op jit(solution)/shard_map/dot_general | solution.py:16
  25.4 0.9 copy-done.5
  26.4 43.8 %reduce-scatter.4.cloned.1.call-done = f32[96,2048]{1,0:T(8,128)} async-done(((f32[384,2048]{1,0:T(8,128)}), f32[96,2048]{1,0:T(8,128)}) %reduce-scatter.4.cloned.1.call-update) | async-done | bytes 786448 | tf_op jit(solution)/shard_map/reduce_scatter | solution.py:15
  70.3 1.3 reduce_max.23
  71.6 17.8 %all-reduce.3 = (f32[96]{0:T(128)S(1)}, f32[96]{0:T(128)S(1)}) all-reduce(bf16[96]{0:T(256)(128)(2,1)S(1)} %reduce_max.24, f32[96]{0:T(128)S(1)} %reduce_max.23), channel_id=1, replica_groups=mesh['layer'=4,'row'=2,'col'=4] {'row','col'}, use_global_device_ids=true, to_apply=%region_6.0 | all-reduce | flops 192 | bytes 1344 | tf_op jit(solution)/shard_map/pmax | solution.py:24
  89.4 1.5 fusion.2
  91.0 14.2 %all-reduce.2 = (f32[96]{0:T(128)}, f32[96]{0:T(128)}) all-reduce(f32[96]{0:T(128)S(1)} %get-tuple-element.10, f32[96]{0:T(128)S(1)} %get-tuple-element.11), channel_id=1, replica_groups=mesh['layer'=4,'row'=2,'col'=4] {'row','col'}, use_global_device_ids=true, to_apply=%region_8.0 | all-reduce | flops 192 | bytes 1536 | tf_op jit(solution)/shard_map/psum | solution.py:27
  106.5 1.1 fusion.6
  107.6 29.8 %all-gather.2.cloned.1.call-done = bf16[384,2048]{1,0:T(8,128)(2,1)} async-done(((bf16[96,2048]{1,0:T(8,128)(2,1)}), bf16[384,2048]{1,0:T(8,128)(2,1)}) %all-gather.2.cloned.1.call-update) | async-done | bytes 1572880 | tf_op jit(solution)/shard_map/all_gather | solution.py:33
  137.4 3.8 %fusion.9 = f32[384,576]{1,0:T(8,128)} fusion(bf16[384,2048]{1,0:T(8,128)(2,1)} %all-gather.2.cloned.1.call-done, bf16[2048,576]{0,1:T(8,128)(2,1)S(1)} %copy-done), kind=kOutput, calls=%fused_computation.19 | convolution fusion | flops 905969664 | bytes 4816896 | tf_op jit(solution)/shard_map/dot_general | solution.py:37
  141.2 3.5 %all-to-all-start.1 = ((f32[4,96,576]{2,1,0:T(8,128)}), f32[4,96,576]{2,1,0:T(8,128)S(1)}, u32[]{:S(2)}, u32[]{:S(2)}) async-start(f32[4,96,576]{2,1,0:T(8,128)} %bitcast.23), calls=%async_computation.2 | async-start | bytes 1966080 | tf_op jit(solution)/shard_map/all_to_all | solution.py:38
  145.9 11.2 %all-to-all-done.1 = f32[4,96,576]{2,1,0:T(8,128)S(1)} async-done(((f32[4,96,576]{2,1,0:T(8,128)}), f32[4,96,576]{2,1,0:T(8,128)S(1)}, u32[]{:S(2)}, u32[]{:S(2)}) %all-to-all-start.1) | async-done | bytes 884768 | tf_op jit(solution)/shard_map/all_to_all | solution.py:38
  157.1 0.9 copy-done.4
  158.0 2.8 %copy.10 = f32[96,4,576]{2,1,0:T(4,128)} copy(f32[96,4,576]{2,0,1:T(8,128)} %bitcast.22) | data formatting | bytes 1769472 | tf_op jit(solution)/shard_map/all_to_all | solution.py:38
  160.9 2.7 %all_to_all.21 = f32[96,2304]{1,0:T(8,128)} reshape(f32[96,4,576]{2,1,0:T(4,128)} %copy.10) | data formatting | bytes 1769472 | tf_op jit(solution)/shard_map/all_to_all | solution.py:38
  163.6 32.7 %fusion = f32[16,2304]{1,0:T(8,128)S(1)} fusion(f32[96,2304]{1,0:T(8,128)} %all_to_all.21), kind=kCustom, calls=%all-reduce-scatter | all-reduce-scatter fusion | flops 294913 | bytes 1032704
  196.3 1.9 collective-permute-start
  198.2 2.4 %collective-permute-start.1 = (f32[12,2304]{1,0:T(8,128)S(1)}, f32[12,2304]{1,0:T(8,128)S(1)}, u32[]{:S(2)}, u32[]{:S(2)}) collective-permute-start(f32[12,2304]{1,0:T(8,128)S(1)} %slice), channel_id=1, source_target_pairs={{0,2},{1,3},{2,4},{3,5},{4,6},{5,7},{8,10},{9,11},{10,12},{11,13},... | collective-permute-start | bytes 331784
  200.6 5.0 %fusion.8 = f32[2048,576]{0,1:T(8,128)} fusion(bf16[384,2048]{1,0:T(8,128)(2,1)} %all-gather.2.cloned.1.call-done, bf16[384,576]{1,0:T(8,128)(2,1)S(1)} %bitcast.21), kind=kOutput, calls=%fused_computation.18 | convolution fusion | flops 905969664 | bytes 6733824 | tf_op jit(solution)/shard_map/dot_general | solution.py:34
  205.7 2.0 collective-permute-done.1
  208.1 0.7 constant_dynamic-slice_fusion
  (24 shorter events, 2.8 us)
Async XLA Ops:
  7.2 15.1 %copy-start = (bf16[2048,576]{0,1:T(8,128)(2,1)S(1)}, bf16[2048,576]{0,1:T(8,128)(2,1)}, u32[]{:S(2)}) copy-start(bf16[2048,576]{0,1:T(8,128)(2,1)} %param.4) | copy-start | bytes 7077892
  7.2 63.1 %reduce-scatter.4.cloned.1.call-start = ((), (), s32[]{:S(2)}) async-start(), calls=%async_computation.3 | async-start | bytes 3932160 | tf_op jit(solution)/shard_map/reduce_scatter | solution.py:15
  21.4 0.8 copy-start.2
  25.3 1.0 copy-start.5
  25.3 112.1 %all-gather.2.cloned.1.call-start = ((), (), s32[]{:S(2)}) async-start(), calls=%async_computation.4 | async-start | bytes 1966080 | tf_op jit(solution)/shard_map/all_gather | solution.py:33
  70.3 36.2 %copy-start.1 = (f32[96,2048]{1,0:T(8,128)S(1)}, f32[96,2048]{1,0:T(8,128)}, u32[]{:S(2)}) copy-start(f32[96,2048]{1,0:T(8,128)} %reduce-scatter.4.cloned.1.call-done) | copy-start | bytes 2359300
  107.6 37.1 %copy-start.6 = (u32[32]{0:T(128)S(1)}, u32[32]{0:T(128)}, u32[]{:S(2)}) copy-start(u32[32]{0:T(128)} %constant.10) | copy-start | bytes 388
  141.2 15.9 %all-to-all-start.1 = ((f32[4,96,576]{2,1,0:T(8,128)}), f32[4,96,576]{2,1,0:T(8,128)S(1)}, u32[]{:S(2)}, u32[]{:S(2)}) async-start(f32[4,96,576]{2,1,0:T(8,128)} %bitcast.23), calls=%async_computation.2 | async-start | bytes 1966080 | tf_op jit(solution)/shard_map/all_to_all | solution.py:38
  157.1 0.9 copy-start.4
  158.0 42.6 %copy-start.3 = (bf16[4,96,576]{2,1,0:T(8,128)(2,1)S(1)}, bf16[4,96,576]{2,1,0:T(8,128)(2,1)}, u32[]{:S(2)}) copy-start(bf16[4,96,576]{2,1,0:T(8,128)(2,1)} %copy-done.2) | copy-start | bytes 1327108
  196.3 11.4 %collective-permute-start = (f32[16,2304]{1,0:T(8,128)S(1)}, f32[16,2304]{1,0:T(8,128)S(1)}, u32[]{:S(2)}, u32[]{:S(2)}) collective-permute-start(f32[16,2304]{1,0:T(8,128)S(1)} %fusion), channel_id=1, source_target_pairs={{0,1},{1,2},{2,3},{3,4},{4,5},{5,6},{6,7},{8,9},{9,10},{10,11},{11... | collective-permute-start | bytes 442376
  198.2 9.5 %collective-permute-start.1 = (f32[12,2304]{1,0:T(8,128)S(1)}, f32[12,2304]{1,0:T(8,128)S(1)}, u32[]{:S(2)}, u32[]{:S(2)}) collective-permute-start(f32[12,2304]{1,0:T(8,128)S(1)} %slice), channel_id=1, source_target_pairs={{0,2},{1,3},{2,4},{3,5},{4,6},{5,7},{8,10},{9,11},{10,12},{11,13},... | collective-permute-start | bytes 331784
Sparse Core Ops, SparseCore 0:
  25.4 44.7 reduce-scatter.3
  107.7 29.6 all-gather.1
